TPU v7x, 256 devices: a whole 4x4x8 slice. The times are simulated.
256 devices in a mesh: unit: 2 (over core), block: 32 (over z, y), lane: 4 (over x).
Axes of the slice: x: 4, y: 4, z: 8, core: 2. Of those that a mesh axis runs over, the one named last changes fastest.
Arguments:
- image_rows: bfloat16 [16384, 512], P(('unit', 'block', 'lane')), parts along dimension 0, may hold values from -6 to 6, as said below
- text_rows: bfloat16 [16384, 512], P(('unit', 'block', 'lane')), parts along dimension 0, may hold values from -6 to 6, as said below
Outputs:
- image_loss: float32 [16384], P(('unit', 'block', 'lane')), parts along dimension 0
- text_loss: float32 [16384], P(('unit', 'block', 'lane')), parts along dimension 0
- image_grad: float32 [16384, 512], P(('unit', 'block', 'lane')), parts along dimension 0
- text_grad: float32 [16384, 512], P(('unit', 'block', 'lane')), parts along dimension 0
There are 2 independent parts, one for each index of `unit`. A program takes and returns all parts, laid end to end along the dimension named above; each array names one. Nothing has to cross between parts.
Inputs may be any that keep to these rules, and one draw needn't show every extreme that they name: image_rows holds numbers from -6 to 6. text_rows holds numbers from -6 to 6.
All inputs are finite; a program needn't handle non-finite values.
Results may differ from a plain program's by a relative error of at most 0.0035.
Values may be sent and summed in bfloat16 or wider, within the bound.
A program may use at most 64 MiB of HBM per device.

v0:
```python
import functools

import jax
import jax.numpy as jnp
from jax import lax
from jax.experimental import pallas as pl
from jax.experimental.pallas import tpu as pltpu
from jax.sharding import PartitionSpec as P

NT = (((1,), (1,)), ((), ()))


def unit_rows(values):
    wide = values.astype(jnp.float32)
    scale = lax.rsqrt(jnp.sum(wide * wide, axis=-1, keepdims=True) + 1e-06)
    return (wide * scale).astype(jnp.bfloat16)


def upright(row):
    return jnp.transpose(jnp.broadcast_to(row, (8, row.shape[1])))[:, :1]


def own_piece(row, pieces, mine):
    size = row.shape[1] // pieces
    return sum(
        jnp.where(mine == piece, row[:, piece * size : (piece + 1) * size], 0.0)
        for piece in range(pieces)
    )


def kernel(
    lanes,
    blocks,
    group,
    image_hbm,
    text_hbm,
    image_loss,
    text_loss,
    image_grad,
    text_grad,
    image_raw,
    text_raw,
    images,
    texts,
    power,
    power_t,
    row_mine,
    row_in,
    col_mine,
    col_in,
    image_acc,
    image_out,
    image_in,
    text_out,
    text_in,
    text_own,
    load_sem,
    send_image,
    recv_image,
    send_text,
    recv_text,
    send_row,
    recv_row,
    send_col,
    recv_col,
    send_ig,
    recv_ig,
    send_tg,
    recv_tg,
):
    lane, block = lax.axis_index("lane"), lax.axis_index("block")
    rows = image_raw.shape[0]
    images_n, texts_n = lanes * rows, blocks * rows
    groups = texts_n // group
    per_group = group // rows

    loads = [
        pltpu.make_async_copy(image_hbm, image_raw, load_sem.at[0]),
        pltpu.make_async_copy(text_hbm, text_raw, load_sem.at[1]),
    ]
    for load in loads:
        load.start()
    barrier = pltpu.get_barrier_semaphore()
    for k in range(1, blocks):
        pl.semaphore_signal(barrier, inc=1, device_id={"block": lax.rem(block + k, blocks)})
    for k in range(1, lanes):
        pl.semaphore_signal(barrier, inc=1, device_id={"lane": lax.rem(lane + k, lanes)})

    my_image = pl.ds(pl.multiple_of(lane * rows, rows), rows)
    my_text = pl.ds(pl.multiple_of(block * rows, rows), rows)
    loads[1].wait()
    texts[my_text, :] = unit_rows(text_raw[...])
    loads[0].wait()
    images[my_image, :] = unit_rows(image_raw[...])
    pl.semaphore_wait(barrier, lanes + blocks - 2)

    def to_block(k, src, dst, send, recv):
        return pltpu.make_async_remote_copy(
            src_ref=src,
            dst_ref=dst,
            send_sem=send.at[k - 1],
            recv_sem=recv.at[k - 1],
            device_id={"block": lax.rem(block + k, blocks)},
        )

    def to_lane(k, src, dst, send, recv):
        return pltpu.make_async_remote_copy(
            src_ref=src,
            dst_ref=dst,
            send_sem=send.at[k - 1],
            recv_sem=recv.at[k - 1],
            device_id={"lane": lax.rem(lane + k, lanes)},
        )

    text_copies = [
        to_block(k, texts.at[my_text], texts.at[my_text], send_text, recv_text)
        for k in range(1, blocks)
    ]
    image_copies = [
        to_lane(k, images.at[my_image], images.at[my_image], send_image, recv_image)
        for k in range(1, lanes)
    ]
    for copy in text_copies + image_copies:
        copy.start()

    pair = 12.0 * lax.dot_general(
        images[my_image, :], texts[my_text, :], NT, preferred_element_type=jnp.float32
    )
    eye = lax.broadcasted_iota(jnp.int32, (rows, rows), 0) == lax.broadcasted_iota(
        jnp.int32, (rows, rows), 1
    )
    matched = jnp.sum(jnp.where(eye, pair, 0.0), axis=0, keepdims=True)

    for copy in image_copies + text_copies:
        copy.wait_recv()

    def over_groups(step, start):
        if groups == 1:
            return step(0, start)
        return lax.fori_loop(0, groups, step, start)

    def group_rows(g):
        return pl.ds(g * group if groups == 1 else pl.multiple_of(g * group, group), group)

    def power_step(g, row_sum):
        some = texts[group_rows(g), :]
        p = jnp.exp(12.0 * lax.dot_general(images[...], some, NT, preferred_element_type=jnp.float32))
        q = jnp.exp(12.0 * lax.dot_general(some, images[...], NT, preferred_element_type=jnp.float32))
        power[g] = p
        power_t[g] = q
        col_mine[g] = jnp.sum(p, axis=0, keepdims=True)
        return row_sum + jnp.sum(q, axis=0, keepdims=True)

    row_mine[...] = over_groups(power_step, jnp.zeros((1, images_n), jnp.float32))
    sum_copies = [
        to_block(k, col_mine, col_in.at[k - 1], send_col, recv_col) for k in range(1, blocks)
    ] + [to_lane(k, row_mine, row_in.at[k - 1], send_row, recv_row) for k in range(1, lanes)]
    for copy in sum_copies:
        copy.start()
    for copy in sum_copies:
        copy.wait_recv()

    row_sum = row_mine[...]
    for k in range(1, lanes):
        row_sum = row_sum + row_in[k - 1]
    row_inv = 1.0 / row_sum
    row_inv_up = upright(row_inv)
    image_loss[...] = jnp.log(own_piece(row_sum, lanes, lane)) - matched

    def col_total(g):
        total = col_mine[g]
        for k in range(1, blocks):
            total = total + col_in[k - 1, g]
        return total

    image_acc[...] = jnp.zeros_like(image_acc)

    def grad_step(g, own_col):
        total = col_total(g)
        col_inv = 1.0 / total
        col_inv_up = upright(col_inv)
        first = block - g * per_group
        ids_t = lax.broadcasted_iota(jnp.int32, (group, images_n), 0) - first * rows
        ids_i = lax.broadcasted_iota(jnp.int32, (group, images_n), 1) - lane * rows
        same_t = (ids_t == ids_i) & (ids_i >= 0) & (ids_i < rows)
        pull_t = (power_t[g] * (row_inv + col_inv_up) - jnp.where(same_t, 2.0, 0.0)).astype(
            jnp.bfloat16
        )
        part = jnp.dot(pull_t, images[...], preferred_element_type=jnp.float32)
        text_own[group_rows(g), :] = part
        text_out[group_rows(g), :] = part.astype(jnp.bfloat16)
        ids_i = lax.broadcasted_iota(jnp.int32, (images_n, group), 0) - lane * rows
        ids_t = lax.broadcasted_iota(jnp.int32, (images_n, group), 1) - first * rows
        same = (ids_t == ids_i) & (ids_i >= 0) & (ids_i < rows)
        pull = (power[g] * (row_inv_up + col_inv) - jnp.where(same, 2.0, 0.0)).astype(jnp.bfloat16)
        image_acc[...] += jnp.dot(
            pull, texts[group_rows(g), :], preferred_element_type=jnp.float32
        )
        return own_col + own_piece(total, per_group, first)

    own_col = over_groups(grad_step, jnp.zeros((1, rows), jnp.float32))
    image_out[...] = image_acc[...].astype(jnp.bfloat16)

    def there(index, count, k):
        return pl.ds(pl.multiple_of(lax.rem(index + k, count) * rows, rows), rows)

    tg_copies = [
        to_block(k, text_out.at[there(block, blocks, k)], text_in.at[k - 1], send_tg, recv_tg)
        for k in range(1, blocks)
    ]
    ig_copies = [
        to_lane(k, image_out.at[there(lane, lanes, k)], image_in.at[k - 1], send_ig, recv_ig)
        for k in range(1, lanes)
    ]
    for copy in tg_copies + ig_copies:
        copy.start()
    text_loss[...] = jnp.log(own_col) - matched
    for copy in ig_copies:
        copy.wait_recv()
    grad = image_acc[my_image, :]
    for k in range(1, lanes):
        grad = grad + image_in[k - 1].astype(jnp.float32)
    image_grad[...] = grad
    for copy in tg_copies:
        copy.wait_recv()
    grad = text_own[my_text, :]
    for k in range(1, blocks):
        grad = grad + text_in[k - 1].astype(jnp.float32)
    text_grad[...] = grad
    for copy in text_copies + image_copies + sum_copies + tg_copies + ig_copies:
        copy.wait_send()


def place(*refs):
    sem = refs[-1]
    copies = [
        pltpu.make_async_copy(refs[i], refs[i + 4], sem.at[i]) for i in (2, 3, 0, 1)
    ]
    for copy in copies:
        copy.start()
    for copy in copies:
        copy.wait()


def solution(mesh):
    lanes, blocks = mesh.shape["lane"], mesh.shape["block"]

    def body(image_rows, text_rows):
        rows, width = image_rows.shape
        images_n, texts_n = lanes * rows, blocks * rows
        group = rows * next(c for c in (4, 2, 1) if blocks % c == 0)
        groups = texts_n // group
        f32, bf16 = jnp.float32, jnp.bfloat16
        limit = 4 * (
            images_n * texts_n * 8 + (images_n + texts_n) * width * 6 + rows * width * 64
        )
        limit = min(limit, 60 * 2**20)
        sems = [pltpu.SemaphoreType.DMA((2,))]
        for count in (lanes, blocks, lanes, blocks, lanes, blocks):
            sems += [pltpu.SemaphoreType.DMA((max(count - 1, 1),))] * 2
        image_loss, text_loss, image_grad, text_grad = pl.pallas_call(
            functools.partial(kernel, lanes, blocks, group),
            out_shape=(
                jax.ShapeDtypeStruct((1, rows), f32),
                jax.ShapeDtypeStruct((1, rows), f32),
                jax.ShapeDtypeStruct((rows, width), f32),
                jax.ShapeDtypeStruct((rows, width), f32),
            ),
            in_specs=[pl.BlockSpec(memory_space=pltpu.HBM)] * 2,
            out_specs=[pl.BlockSpec(memory_space=pltpu.VMEM)] * 4,
            scratch_shapes=[
                pltpu.VMEM((rows, width), bf16),
                pltpu.VMEM((rows, width), bf16),
                pltpu.VMEM((images_n, width), bf16),
                pltpu.VMEM((texts_n, width), bf16),
                pltpu.VMEM((groups, images_n, group), f32),
                pltpu.VMEM((groups, group, images_n), f32),
                pltpu.VMEM((1, images_n), f32),
                pltpu.VMEM((max(lanes - 1, 1), 1, images_n), f32),
                pltpu.VMEM((groups, 1, group), f32),
                pltpu.VMEM((max(blocks - 1, 1), groups, 1, group), f32),
                pltpu.VMEM((images_n, width), f32),
                pltpu.VMEM((images_n, width), bf16),
                pltpu.VMEM((max(lanes - 1, 1), rows, width), bf16),
                pltpu.VMEM((texts_n, width), bf16),
                pltpu.VMEM((max(blocks - 1, 1), rows, width), bf16),
                pltpu.VMEM((texts_n, width), f32),
            ]
            + sems,
            compiler_params=pltpu.CompilerParams(
                collective_id=0, has_side_effects=True, vmem_limit_bytes=limit
            ),
        )(*(pltpu.with_memory_space_constraint(x, pltpu.HBM) for x in (image_rows, text_rows)))
        results = (image_loss, text_loss, image_grad, text_grad)
        image_loss, text_loss, image_grad, text_grad = pl.pallas_call(
            place,
            out_shape=tuple(jax.ShapeDtypeStruct(r.shape, r.dtype) for r in results),
            in_specs=[pl.BlockSpec(memory_space=pltpu.VMEM)] * 4,
            out_specs=[pl.BlockSpec(memory_space=pl.ANY)] * 4,
            scratch_shapes=[pltpu.SemaphoreType.DMA((4,))],
            compiler_params=pltpu.CompilerParams(vmem_limit_bytes=4 * rows * width * 8),
        )(*results)
        return (image_loss.reshape(rows), text_loss.reshape(rows), image_grad, text_grad)

    rows_spec = P(("unit", "block", "lane"), None)
    flat_spec = P(("unit", "block", "lane"))
    return jax.shard_map(
        body,
        mesh=mesh,
        in_specs=(rows_spec, rows_spec),
        out_specs=(flat_spec, flat_spec, rows_spec, rows_spec),
        check_vma=False,
    )
```

profile of v0, /device:TPU:2, one launch (start us, length us, event | category | flops | bytes accessed | tf_op | source)
XLA Modules:
  0.0 125.9 jit_solution(1576203881422431701)
XLA Ops:
  0.6 124.5 %shard_map.57 = (f32[1,64]{1,0:T(1,128)S(1)}, f32[1,64]{1,0:T(1,128)S(1)}, f32[64,512]{1,0:T(8,128)S(1)}, f32[64,512]{1,0:T(8,128)S(1)}) custom-call(bf16[64,512]{1,0:T(8,128)(2,1)} %image_hbm.1, bf16[64,512]{1,0:T(8,128)(2,1)} %text_hbm.1), custom_call_target="tpu_custom_call" | custom-call | tf_op jit(solution)/shard_map/pallas_call | solution.py:261
  125.1 0.7 shard_map.58
where the time goes:
time: 128 us; the launch traced here: 126 us
  Pallas kernels  125 us (98%)
    pallas_call x1, Pallas kernels, body(): pl.pallas_call(functools.partial(kernel, lanes, blocks, group), out_shape...  124 us

commit v1 on v0

v1 whole, which is shorter than its diff:
```python
import functools

import jax
import jax.numpy as jnp
from jax import lax
from jax.experimental import pallas as pl
from jax.experimental.pallas import tpu as pltpu
from jax.sharding import PartitionSpec as P

NT = (((1,), (1,)), ((), ()))
F32, BF16 = jnp.float32, jnp.bfloat16

Z_SLOTS = [0, 1, 7, 2, 6, 3, 5, 4]
P_SLOTS = [
    (0, 0), (0, 1), (0, 3), (1, 0), (3, 0), (1, 1), (1, 3), (3, 1),
    (3, 3), (0, 2), (2, 0), (2, 1), (2, 3), (1, 2), (3, 2), (2, 2),
]
Z_NEAR = [2, 6, 1, 7]
Z_FAR = [(3, 0, 2, 2), (5, 0, 2, 6), (4, 0, 1, 2), (4, 1, 1, 6)]
P_NEAR = [(1, 1), (3, 3), (1, 3), (3, 1), (0, 1), (0, 3), (1, 0), (3, 0)]
P_FAR = [
    ((2, 2), 0, 1, (1, 1)), ((2, 2), 1, 1, (3, 3)),
    ((1, 2), 0, 1, (1, 1)), ((1, 2), 1, 1, (1, 3)),
    ((3, 2), 0, 1, (3, 1)), ((3, 2), 1, 1, (3, 3)),
    ((2, 1), 0, 1, (1, 1)), ((2, 1), 1, 1, (3, 1)),
    ((2, 3), 0, 1, (1, 3)), ((2, 3), 1, 1, (3, 3)),
    ((0, 2), 0, 1, (0, 1)), ((0, 2), 1, 1, (0, 3)),
    ((2, 0), 0, 1, (1, 0)), ((2, 0), 1, 1, (3, 0)),
]


class Ring:
    def __init__(self, size, here):
        self.size, self.here = size, here

    def neg(self, a):
        return -a % self.size

    def sub(self, a, b):
        return (a - b) % self.size

    def index(self, a):
        return lax.rem(self.here + a, self.size)


class Line:
    slots, near, far = Z_SLOTS, Z_NEAR, Z_FAR

    def __init__(self, side, z, y):
        self.z, self.y, self.side = Ring(8, z), y, side

    def neg(self, a):
        return self.z.neg(a)

    def sub(self, a, b):
        return self.z.sub(a, b)

    def device(self, a):
        return {"block": self.z.index(a) * self.side + self.y}

    def index(self, a):
        return self.z.index(a)


class Plane:
    slots, near, far = P_SLOTS, P_NEAR, P_FAR

    def __init__(self, side, z, y, x):
        self.z, self.y, self.x, self.side = z, Ring(side, y), Ring(side, x), side

    def neg(self, a):
        return (self.y.neg(a[0]), self.x.neg(a[1]))

    def sub(self, a, b):
        return (self.y.sub(a[0], b[0]), self.x.sub(a[1], b[1]))

    def device(self, a):
        return {"block": self.z * self.side + self.y.index(a[0]), "lane": self.x.index(a[1])}

    def index(self, a):
        return self.y.index(a[0]) * self.side + self.x.index(a[1])


def unit_rows(values):
    wide = values.astype(F32)
    scale = lax.rsqrt(jnp.sum(wide * wide, axis=-1, keepdims=True) + 1e-06)
    return (wide * scale).astype(BF16)


def upright(row):
    return jnp.transpose(jnp.broadcast_to(row, (8, row.shape[1])))[:, :1]


class Side:
    def __init__(self, group, rows, data, sums, mine, own, out, far_in, near_in, sems):
        self.g, self.rows, self.data, self.sums, self.mine = group, rows, data, sums, mine
        self.own, self.out, self.far_in, self.near_in = own, out, far_in, near_in
        self.pos = {slot: k for k, slot in enumerate(group.slots)}
        ag1, ag2, sm, rs1, rs2 = [(sems[2 * k], sems[2 * k + 1]) for k in range(5)]
        g = group

        def remote(src, dst, sem, k, offset):
            return pltpu.make_async_remote_copy(
                src_ref=src, dst_ref=dst, send_sem=sem[0].at[k], recv_sem=sem[1].at[k],
                device_id=g.device(offset),
            )

        self.gather_near = {
            o: remote(data.at[self.rows_of(g.slots[0])], data.at[self.rows_of(g.neg(o))], ag1, k, o)
            for k, o in enumerate(g.near)
        }
        self.gather_far = [
            remote(
                data.at[self.rows_of(g.neg(r), h, n)], data.at[self.rows_of(g.neg(o), h, n)],
                ag2, k, g.sub(o, r),
            )
            for k, (o, h, n, r) in enumerate(g.far)
        ]
        self.exchange = [
            remote(mine, sums.at[k], sm, k, o) for k, o in enumerate(g.slots[1:])
        ]
        self.reduce_far = [
            remote(
                out.at[self.rows_of(g.neg(o), h, n)], far_in.at[k, pl.ds(0, n * rows // 2)],
                rs1, k, g.sub(r, o),
            )
            for k, (o, h, n, r) in enumerate(g.far)
        ]
        self.reduce_near = {
            o: remote(out.at[self.rows_of(g.neg(o))], near_in.at[k], rs2, k, g.neg(o))
            for k, o in enumerate(g.near)
        }

    def rows_of(self, slot, half=0, halves=2):
        return pl.ds(self.pos[slot] * self.rows + half * self.rows // 2, halves * self.rows // 2)

    def start_gather(self):
        for o in self.g.near:
            self.gather_near[o].start()

    def relay_gather(self):
        for o in self.g.near:
            self.gather_near[o].wait_recv()
            for k, (_, _, _, r) in enumerate(self.g.far):
                if r == o:
                    self.gather_far[k].start()

    def finish_gather(self, slots):
        for k, (o, _, _, _) in enumerate(self.g.far):
            if self.g.neg(o) in slots:
                self.gather_far[k].wait_recv()

    def keep_sum(self, position, row):
        slot = self.g.slots[position]
        self.mine[pl.ds(self.g.index(slot), 1), 0 : self.rows] = row

    def start_sums(self):
        for copy in self.exchange:
            copy.start()

    def total(self):
        for copy in self.exchange:
            copy.wait_recv()
        total = self.mine[...]
        for k in range(len(self.exchange)):
            total = total + self.sums[k]
        return total

    def send_far(self, slots):
        for k, (o, _, _, _) in enumerate(self.g.far):
            if self.g.neg(o) in slots:
                self.reduce_far[k].start()

    def send_near(self, o):
        where = self.rows_of(self.g.neg(o))
        added = False
        for k, (_, h, n, r) in enumerate(self.g.far):
            if r == o:
                self.reduce_far[k].wait_recv()
                part = self.rows_of(self.g.neg(o), h, n)
                self.own[part, :] += self.far_in[k, pl.ds(0, n * self.rows // 2)].astype(F32)
                added = True
        if added:
            self.out[where, :] = self.own[where, :].astype(BF16)
        self.reduce_near[o].start()

    def gradient(self):
        for o in self.g.near:
            self.reduce_near[o].wait_recv()
        grad = self.own[self.rows_of(self.g.slots[0]), :]
        for k in range(len(self.g.near)):
            grad = grad + self.near_in[k].astype(F32)
        return grad

    def wait_sends(self):
        for copies in (
            list(self.gather_near.values()), self.gather_far, self.exchange,
            self.reduce_far, list(self.reduce_near.values()),
        ):
            for copy in copies:
                copy.wait_send()


def kernel(
    side, group,
    image_hbm, text_hbm,
    image_loss, text_loss, image_grad, text_grad,
    image_raw, text_raw, images, texts, power, power_t,
    row_mine, row_in, col_mine, col_in, row_tot, col_tot, row_all, col_all,
    image_own, text_own, image_out, text_out,
    image_far, text_far, image_near, text_near,
    load_sem, *sems,
):
    lane, block = lax.axis_index("lane"), lax.axis_index("block")
    z, y = block // side, lax.rem(block, side)
    rows = image_raw.shape[0]
    per = group // rows
    image = Side(Line(side, z, y), rows, images, row_in, row_mine, image_own, image_out, image_far, image_near, sems[:10])
    text = Side(Plane(side, z, y, lane), rows, texts, col_in, col_mine, text_own, text_out, text_far, text_near, sems[10:])
    image_groups, text_groups = len(Z_SLOTS) // per, len(P_SLOTS) // per

    loads = [
        pltpu.make_async_copy(image_hbm, image_raw, load_sem.at[0]),
        pltpu.make_async_copy(text_hbm, text_raw, load_sem.at[1]),
    ]
    for load in loads:
        load.start()
    barrier = pltpu.get_barrier_semaphore()
    for part in (image, text):
        for o in part.g.near:
            pl.semaphore_signal(barrier, inc=1, device_id=part.g.device(o))

    loads[1].wait()
    texts[0:rows, :] = unit_rows(text_raw[...])
    loads[0].wait()
    images[0:rows, :] = unit_rows(image_raw[...])
    pl.semaphore_wait(barrier, len(Z_NEAR) + len(P_NEAR))
    text.start_gather()
    image.start_gather()

    pair = 12.0 * lax.dot_general(images[0:rows, :], texts[0:rows, :], NT, preferred_element_type=F32)
    eye = lax.broadcasted_iota(jnp.int32, (rows, rows), 0) == lax.broadcasted_iota(jnp.int32, (rows, rows), 1)
    matched = jnp.sum(jnp.where(eye, pair, 0.0), axis=0, keepdims=True)

    image.relay_gather()
    text.relay_gather()

    def some(g):
        return pl.ds(g * group, group)

    row_sums, col_sums = [0.0] * image_groups, [0.0] * text_groups

    def powers(h, g):
        i, t = images[some(h), :], texts[some(g), :]
        p = jnp.exp(12.0 * lax.dot_general(i, t, NT, preferred_element_type=F32))
        q = jnp.exp(12.0 * lax.dot_general(t, i, NT, preferred_element_type=F32))
        power[some(h), some(g)] = p
        power_t[some(g), some(h)] = q
        col_sums[g] += jnp.sum(p, axis=0, keepdims=True)
        row_sums[h] += jnp.sum(q, axis=0, keepdims=True)

    powers(0, 0)
    powers(0, 1)
    image.finish_gather(Z_SLOTS)
    powers(1, 0)
    powers(1, 1)
    text.finish_gather(P_SLOTS[2 * per : 3 * per])
    powers(0, 2)
    powers(1, 2)
    text.finish_gather(P_SLOTS[3 * per :])
    powers(0, 3)
    powers(1, 3)

    for part, sums in ((image, row_sums), (text, col_sums)):
        for g, row in enumerate(sums):
            for k in range(per):
                part.keep_sum(g * per + k, row[:, k * rows : (k + 1) * rows])
        part.start_sums()

    def inverse(part, totals, lines):
        totals[...] = 1.0 / part.total()
        for k, slot in enumerate(part.g.slots):
            lines[:, k * rows : (k + 1) * rows] = totals[pl.ds(part.g.index(slot), 1), 0:rows]

    inverse(image, row_tot, row_all)
    inverse(text, col_tot, col_all)
    row_inv, col_inv = row_all[...], col_all[...]
    row_inv_up, col_inv_up = upright(row_inv), upright(col_inv)
    image_loss[...] = -jnp.log(row_inv[:, 0:rows]) - matched
    text_loss[...] = -jnp.log(col_inv[:, 0:rows]) - matched

    def own_two(values):
        ids = [lax.broadcasted_iota(jnp.int32, values.shape, d) for d in (0, 1)]
        return values - jnp.where((ids[0] == ids[1]) & (ids[0] < rows), 2.0, 0.0)

    def text_part(g):
        here = some(g)
        pull = power_t[here, :] * (row_inv + col_inv_up[g * group : (g + 1) * group])
        pull = (own_two(pull) if g == 0 else pull).astype(BF16)
        part = jnp.dot(pull, images[...], preferred_element_type=F32)
        text_own[here, :] = part
        text_out[here, :] = part.astype(BF16)
        text.send_far(P_SLOTS[g * per : (g + 1) * per])

    def image_part(h):
        here = some(h)
        pull = power[here, :] * (row_inv_up[h * group : (h + 1) * group] + col_inv)
        pull = (own_two(pull) if h == 0 else pull).astype(BF16)
        part = jnp.dot(pull, texts[...], preferred_element_type=F32)
        image_own[here, :] = part
        image_out[here, :] = part.astype(BF16)
        image.send_far(Z_SLOTS[h * per : (h + 1) * per])

    text_part(3)
    image_part(1)
    text_part(2)
    text_part(1)
    image_part(0)
    for o in (1, 7, 2, 6):
        image.send_near(o)
    text_part(0)
    for o in P_NEAR:
        text.send_near(o)
    image_grad[...] = image.gradient()
    text_grad[...] = text.gradient()
    image.wait_sends()
    text.wait_sends()


def place(*refs):
    sem = refs[-1]
    copies = [
        pltpu.make_async_copy(refs[i], refs[i + 4], sem.at[i]) for i in (2, 3, 0, 1)
    ]
    for copy in copies:
        copy.start()
    for copy in copies:
        copy.wait()


def solution(mesh):
    side = mesh.shape["lane"]

    def body(image_rows, text_rows):
        rows, width = image_rows.shape
        nz, npl = len(Z_SLOTS), len(P_SLOTS)
        images_n, texts_n = nz * rows, npl * rows
        group = 4 * rows
        scratch = [
            pltpu.VMEM((rows, width), BF16),
            pltpu.VMEM((rows, width), BF16),
            pltpu.VMEM((images_n, width), BF16),
            pltpu.VMEM((texts_n, width), BF16),
            pltpu.VMEM((images_n, texts_n), F32),
            pltpu.VMEM((texts_n, images_n), F32),
            pltpu.VMEM((nz, 128), F32),
            pltpu.VMEM((nz - 1, nz, 128), F32),
            pltpu.VMEM((npl, 128), F32),
            pltpu.VMEM((npl - 1, npl, 128), F32),
            pltpu.VMEM((nz, 128), F32),
            pltpu.VMEM((npl, 128), F32),
            pltpu.VMEM((1, images_n), F32),
            pltpu.VMEM((1, texts_n), F32),
            pltpu.VMEM((images_n, width), F32),
            pltpu.VMEM((texts_n, width), F32),
            pltpu.VMEM((images_n, width), BF16),
            pltpu.VMEM((texts_n, width), BF16),
            pltpu.VMEM((len(Z_FAR), rows, width), BF16),
            pltpu.VMEM((len(P_FAR), rows // 2, width), BF16),
            pltpu.VMEM((len(Z_NEAR), rows, width), BF16),
            pltpu.VMEM((len(P_NEAR), rows, width), BF16),
            pltpu.SemaphoreType.DMA((2,)),
        ]
        for near, far, all_ in ((len(Z_NEAR), len(Z_FAR), nz), (len(P_NEAR), len(P_FAR), npl)):
            for count in (near, far, all_ - 1, far, near):
                scratch += [pltpu.SemaphoreType.DMA((count,))] * 2
        results = pl.pallas_call(
            functools.partial(kernel, side, group),
            out_shape=(
                jax.ShapeDtypeStruct((1, rows), F32),
                jax.ShapeDtypeStruct((1, rows), F32),
                jax.ShapeDtypeStruct((rows, width), F32),
                jax.ShapeDtypeStruct((rows, width), F32),
            ),
            in_specs=[pl.BlockSpec(memory_space=pltpu.HBM)] * 2,
            out_specs=[pl.BlockSpec(memory_space=pltpu.VMEM)] * 4,
            scratch_shapes=scratch,
            compiler_params=pltpu.CompilerParams(
                collective_id=0, has_side_effects=True, vmem_limit_bytes=40 * 2**20
            ),
        )(*(pltpu.with_memory_space_constraint(x, pltpu.HBM) for x in (image_rows, text_rows)))
        image_loss, text_loss, image_grad, text_grad = pl.pallas_call(
            place,
            out_shape=tuple(jax.ShapeDtypeStruct(r.shape, r.dtype) for r in results),
            in_specs=[pl.BlockSpec(memory_space=pltpu.VMEM)] * 4,
            out_specs=[pl.BlockSpec(memory_space=pl.ANY)] * 4,
            scratch_shapes=[pltpu.SemaphoreType.DMA((4,))],
            compiler_params=pltpu.CompilerParams(vmem_limit_bytes=4 * rows * width * 8),
        )(*results)
        return (image_loss.reshape(rows), text_loss.reshape(rows), image_grad, text_grad)

    rows_spec = P(("unit", "block", "lane"), None)
    flat_spec = P(("unit", "block", "lane"))
    return jax.shard_map(
        body,
        mesh=mesh,
        in_specs=(rows_spec, rows_spec),
        out_specs=(flat_spec, flat_spec, rows_spec, rows_spec),
        check_vma=False,
    )
```

time: 128 us -> 41.5 us (0.32); the launches traced: 126 us -> 41.3 us
  Pallas kernels: 125 us -> 40.7 us
    pallas_call x1, Pallas kernels: 124 us -> 40 us  [body(): pl.pallas_call(functools.partial(kernel, side, group), out_shape=(jax.Sha...]
where the time goes in v1:
time: 41.5 us; the launch traced here: 41.3 us
  Pallas kernels  40.7 us (98%)
  between operations  0.64 us (2%)
    pallas_call x1, Pallas kernels, body(): pl.pallas_call(functools.partial(kernel, side, group), out_shape=(jax.Sha...  40 us

profile of v1, /device:TPU:2, one launch (start us, length us, event | category | flops | bytes accessed | tf_op | source)
XLA Modules:
  0.0 41.3 jit_solution(14132503681825654192)
XLA Ops:
  0.6 40.0 %shard_map.57 = (f32[1,64]{1,0:T(1,128)S(1)}, f32[1,64]{1,0:T(1,128)S(1)}, f32[64,512]{1,0:T(8,128)S(1)}, f32[64,512]{1,0:T(8,128)S(1)}) custom-call(bf16[64,512]{1,0:T(8,128)(2,1)} %image_hbm.1, bf16[64,512]{1,0:T(8,128)(2,1)} %text_hbm.1), custom_call_target="tpu_custom_call" | custom-call | tf_op jit(solution)/shard_map/pallas_call | solution.py:377
  40.6 0.7 %shard_map.58 = (f32[1,64]{1,0:T(1,128)}, f32[1,64]{1,0:T(1,128)}, f32[64,512]{1,0:T(8,128)}, f32[64,512]{1,0:T(8,128)}) custom-call(f32[1,64]{1,0:T(1,128)S(1)} %get-tuple-element.12.refs_0_, f32[1,64]{1,0:T(1,128)S(1)} %get-tuple-element.13.refs_1_, f32[64,512]{1,0:T(8,128)S(1)} %get-tuple-element.14.refs_2_, f32[64,512]{1,0:T(8,128)S(1)} %get-tuple-element.15.refs_3_), custom_call_target="tpu_custom_call" | custom-call | tf_op jit(solution)/shard_map/pallas_call | solution.py:392
